TPU v7x, 32 devices: a whole 2x2x4 slice. The times are simulated.
32 devices in a mesh: dp: 2 (over y), row: 4 (over x, core), col: 4 (over z).
Axes of the slice: x: 2, y: 2, z: 4, core: 2. Of those that a mesh axis runs over, the one named last changes fastest.
Arguments:
- tokens: bfloat16 [2048, 8192], P(('dp', 'col'), 'row'), may hold values from -6 to 6
- frozen_weight: bfloat16 [8192, 8192], P('row', 'col'), may hold values from -0.0625 to 0.0625
- input_adapter_factor: bfloat16 [16, 8192], P(None, 'row'), may hold values from -0.0625 to 0.0625
- output_adapter_factor: bfloat16 [16, 8192], P(None, 'col'), may hold values from -1.5 to 1.5
- magnitude: float32 [8192], P('col'), may hold values from 0.5 to 2
- cotangent: bfloat16 [2048, 8192], P(('dp', 'row'), 'col'), may hold values from -6 to 6
- sequence_lengths: int32 [2, 8], P('dp'), may hold values from 1 to 512, 1024 in all within a row
Outputs:
- projected: bfloat16 [2048, 8192], P(('dp', 'row'), 'col')
- grad_mag: float32 [8192], P('col')
- input_factor_gradient: float32 [16, 8192], P(None, 'row')
- grad_b: float32 [16, 8192], P(None, 'col')
Inputs may be any that keep to these rules, and one draw needn't show every extreme that they name: `sequence_lengths`: each group's 8 lengths sum to 1024, and one of them is exactly 512.
All inputs are finite; a program needn't handle non-finite values.
Results may differ from a plain program's by a relative error of at most 0.0052.
Values may be sent and summed in bfloat16 or wider, within the bound.
No kernel may reach another device: no remote copies, remote signals or barrier semaphores. Data moves between devices by JAX's collectives and lax.ppermute only.
A program may use at most 64 MiB of HBM per device.

v0:
```python
import jax
import jax.numpy as jnp
from jax import lax
from jax.sharding import PartitionSpec as P

norm_eps = 1e-06
highest_precision = lax.Precision.HIGHEST


def contract_product(left, right, left_dim, right_dim):
    return lax.dot_general(
        left, right, (((left_dim,), (right_dim,)), ((), ())), preferred_element_type=jnp.float32
    )


def per_device(
    tokens,
    frozen_weight,
    input_adapter_factor,
    output_adapter_factor,
    magnitude,
    cotangent,
    sequence_lengths,
):
    row_count = lax.axis_size("row")
    col_count = lax.axis_size("col")
    row_index = lax.axis_index("row")
    col_index = lax.axis_index("col")
    group_index = lax.axis_index("dp")
    local_rows = tokens.shape[0]
    group_rows = local_rows * col_count
    block_rows = group_rows // row_count
    adapter_rank_size = input_adapter_factor.shape[0]
    low_rank_update = contract_product(input_adapter_factor, output_adapter_factor, 0, 0)
    merged = frozen_weight.astype(jnp.float32) + low_rank_update
    norm_terms = jnp.sum(merged * merged, axis=0)
    gram_partial_terms = contract_product(input_adapter_factor, input_adapter_factor, 1, 1)
    merged_factor_terms = jnp.dot(
        input_adapter_factor, frozen_weight, preferred_element_type=jnp.float32
    ) + jnp.dot(
        gram_partial_terms, output_adapter_factor.astype(jnp.float32), precision=highest_precision
    )
    portion = lax.all_gather(tokens, "col", axis=0, tiled=True)
    base_piece = jnp.dot(portion, frozen_weight, preferred_element_type=jnp.float32)
    down_portion = contract_product(portion, input_adapter_factor, 1, 1)
    frozen_rows, down_rows = (
        lax.psum_scatter(base_piece, "row", scatter_dimension=0, tiled=True),
        lax.psum_scatter(down_portion, "row", scatter_dimension=0, tiled=True),
    )
    norm_sq, merged_input_factor = lax.psum((norm_terms, merged_factor_terms), "row")
    down_activations = down_rows.astype(jnp.bfloat16)
    col_norm = jnp.sqrt(norm_sq + norm_eps)
    col_scale = magnitude / col_norm
    query_projection = frozen_rows + jnp.dot(
        down_activations, output_adapter_factor, preferred_element_type=jnp.float32
    )
    projected = (query_projection * col_scale[None, :]).astype(jnp.bfloat16)
    lengths = sequence_lengths[0]
    ends = jnp.cumsum(lengths, dtype=jnp.int32)
    starts = ends - lengths
    positions = row_index * block_rows + jnp.arange(block_rows, dtype=jnp.int32)
    inside = (positions[:, None] >= starts[None, :]) & (positions[:, None] < ends[None, :])
    inverse = 1.0 / lengths.astype(jnp.float32)
    weights = jnp.sum(jnp.where(inside, inverse[None, :], jnp.float32(0.0)), axis=1)
    grad_out = cotangent.astype(jnp.float32) * weights[:, None]
    scale_terms = jnp.sum(grad_out * query_projection, axis=0)
    projection_gradient = (grad_out * col_scale[None, :]).astype(jnp.bfloat16)
    bgrad_terms = contract_product(down_activations, projection_gradient, 0, 0)
    scale_grad, bgrad_data = lax.psum((scale_terms, bgrad_terms), ("dp", "row"))
    grad_mag = scale_grad / col_norm
    norm_coefficient = -scale_grad * magnitude / (col_norm * col_norm * col_norm)
    grad_b = bgrad_data + merged_input_factor * norm_coefficient[None, :]
    backward_terms = contract_product(projection_gradient, output_adapter_factor, 1, 1)
    padded = lax.dynamic_update_slice_in_dim(
        jnp.zeros((group_rows, adapter_rank_size), jnp.float32),
        backward_terms,
        row_index * block_rows,
        0,
    )
    backward_rows = lax.psum(padded, ("row", "col")).astype(jnp.bfloat16)
    back_mine = lax.dynamic_slice_in_dim(backward_rows, col_index * local_rows, local_rows, 0)
    row_term = contract_product(back_mine, tokens, 0, 0)
    scaled_output_factor = (
        output_adapter_factor.astype(jnp.float32) * norm_coefficient[None, :]
    ).astype(jnp.bfloat16)
    norm_term = contract_product(scaled_output_factor, frozen_weight, 1, 1) + jnp.dot(
        contract_product(scaled_output_factor, output_adapter_factor, 1, 1),
        input_adapter_factor.astype(jnp.float32),
        precision=highest_precision,
    )
    first_group = (group_index == 0).astype(jnp.float32)
    input_factor_gradient = lax.psum(row_term + first_group * norm_term, ("dp", "col"))
    return (projected, grad_mag, input_factor_gradient, grad_b)


def solution(mesh):
    in_specs = (
        P(("dp", "col"), "row"),
        P("row", "col"),
        P(None, "row"),
        P(None, "col"),
        P("col"),
        P(("dp", "row"), "col"),
        P("dp", None),
    )
    out_specs = (P(("dp", "row"), "col"), P("col"), P(None, "row"), P(None, "col"))
    return jax.shard_map(
        per_device, mesh=mesh, in_specs=in_specs, out_specs=out_specs, check_vma=False
    )
```

profile of v0, /device:TPU:0, one launch (start us, length us, event | category | flops | bytes accessed | tf_op | source)
XLA Modules:
  0.0 366.2 jit_solution(13270679273868545477)
XLA Ops:
  7.2 0.0 copy-start
  7.2 0.0 all-gather.2.cloned.1.call-start
  7.2 0.7 all-gather.2.cloned.1.call-update
  7.9 0.0 reduce-scatter.5.cloned.1.call-start
  8.0 85.1 %all-gather.2.cloned.1.call-done = bf16[1024,2048]{1,0:T(8,128)(2,1)} async-done(((bf16[256,2048]{1,0:T(8,128)(2,1)}), bf16[1024,2048]{1,0:T(8,128)(2,1)}) %all-gather.2.cloned.1.call-update) | async-done | bytes 4194320 | tf_op jit(solution)/shard_map/all_gather | solution.py:43
  93.1 0.0 copy-done
  93.1 4.0 %fusion.14 = f32[1024,16]{0,1:T(8,128)} fusion(bf16[1024,2048]{1,0:T(8,128)(2,1)} %all-gather.2.cloned.1.call-done, bf16[16,2048]{1,0:T(8,128)(2,1)S(1)} %copy-done), kind=kOutput, calls=%fused_computation.33 | convolution fusion | flops 67108864 | bytes 4325376 | tf_op jit(solution)/shard_map/dot_general | solution.py:11
  97.1 0.0 reduce-scatter.5.cloned.1.call-update
  97.1 0.0 reduce-scatter.3.cloned.1.call-start
  97.1 14.4 %fusion.13 = f32[1024,2048]{1,0:T(8,128)} fusion(bf16[1024,2048]{1,0:T(8,128)(2,1)} %all-gather.2.cloned.1.call-done, bf16[2048,2048]{1,0:T(8,128)(2,1)} %param.8), kind=kOutput, calls=%fused_computation.32 | convolution fusion | flops 8589934592 | bytes 20971520 | tf_op jit(solution)/shard_map/dot_general | solution.py:44
  111.6 0.0 reduce-scatter.3.cloned.1.call-update
  111.6 0.0 all-reduce.8.cloned.1.call-start
  111.6 0.1 fusion.16
  111.8 4.6 %fusion.15 = f32[16,2048]{1,0:T(8,128)S(1)} fusion(bf16[16,2048]{1,0:T(8,128)(2,1)S(1)} %copy-done, bf16[2048,2048]{1,0:T(8,128)(2,1)} %param.8), kind=kOutput, calls=%fused_computation.34 | convolution fusion | flops 134217728 | bytes 8585216 | tf_op jit(solution)/shard_map/dot_general | solution.py:38
  116.4 0.0 copy-done.2
  116.4 0.9 convolution_add_fusion.1
  117.3 0.0 all-reduce.8.cloned.1.call-update
  117.3 0.0 all-reduce.6.cloned.1.call-start
  117.3 0.0 copy-start.5
  117.4 0.0 copy-start.4
  117.4 0.0 copy-start.3
  117.4 5.9 %multiply_reduce_fusion = f32[2048]{0:T(1024)S(1)} fusion(bf16[2048,2048]{1,0:T(8,128)(2,1)} %param.8, bf16[16,2048]{1,0:T(8,128)(2,1)S(1)} %copy-done, bf16[16,2048]{1,0:T(8,128)(2,1)S(1)} %copy-done.2), kind=kOutput, calls=%fused_computation | convolution fusion | flops 150992896 | bytes 8527872 | tf_op jit(solution)/shard_map/dot_general | solution.py:11
  123.3 0.0 copy-done.5
  123.3 0.2 reduce-window.4
  123.5 6.5 %psum.42 = f32[2048]{0:T(1024)S(1)} all-reduce(f32[2048]{0:T(1024)S(1)} %multiply_reduce_fusion), channel_id=1, replica_groups=mesh['dp'=2,'row'=4,'col'=4] {'row'}, use_global_device_ids=true, to_apply=%region_3.0 | all-reduce | flops 2048 | bytes 16384 | tf_op jit(solution)/shard_map/psum | solution.py:50
  130.0 0.0 copy-done.4
  130.1 0.1 select_reduce_fusion
  130.2 0.5 convolution_dynamic-update-slice_fusion
  130.7 69.2 %psum.44 = bf16[1024,16]{1,0:T(8,128)(2,1)S(1)} all-reduce(f32[1024,16]{1,0:T(8,128)S(1)} %convolution_dynamic-update-slice_fusion), channel_id=1, replica_groups=mesh['dp'=2,'row'=4,'col'=4] {'row','col'}, use_global_device_ids=true, to_apply=%region_8.9 | all-reduce | flops 16384 | bytes 98304 | tf_op jit(solution)/shard_map/psum | solution.py:80
  199.9 0.0 reduce-scatter.5.cloned.1.call-done
  200.0 1.8 fusion.1
  201.8 0.0 all-reduce.6.cloned.1.call-update
  201.8 0.0 all-reduce.4.cloned.1.call-start
  201.8 0.0 reduce-scatter.3.cloned.1.call-done
  201.9 3.2 multiply_reduce_fusion.1
  205.1 12.1 %psum.43 = f32[2048]{0:T(1024)S(1)} all-reduce(f32[2048]{0:T(1024)S(1)} %get-tuple-element.4), channel_id=1, replica_groups=mesh['dp'=2,'row'=4,'col'=4] {'dp','row'}, use_global_device_ids=true, to_apply=%region_7.8 | all-reduce | flops 2048 | bytes 16384 | tf_op jit(solution)/shard_map/psum | solution.py:69
  217.1 0.6 fusion.6
  217.8 5.7 %fusion.3 = f32[16,2048]{1,0:T(8,128)S(1)} fusion(bf16[2048,2048]{1,0:T(8,128)(2,1)} %param.8, bf16[16,2048]{1,0:T(8,128)(2,1)S(1)} %copy-done.2, f32[2048]{0:T(1024)S(1)} %get-tuple-element.6), kind=kOutput, calls=%fused_computation.16 | convolution fusion | flops 134316032 | bytes 8593408 | tf_op jit(solution)/shard_map/dot_general | solution.py:11
  223.5 0.1 fusion.2
  223.6 0.2 fusion
  223.9 0.0 copy-done.1
  223.9 0.9 convolution_add_fusion.3
  224.8 0.0 all-reduce.4.cloned.1.call-update
  224.8 2.4 all-reduce.8.cloned.1.call-done
  227.2 57.0 %all-reduce.6.cloned.1.call-done = f32[16,2048]{1,0:T(8,128)} async-done(((f32[16,2048]{1,0:T(8,128)}), f32[16,2048]{1,0:T(8,128)}) %all-reduce.6.cloned.1.call-update) | async-done | bytes 131088 | tf_op jit(solution)/shard_map/psum | solution.py:69
  284.2 1.6 multiply_add_fusion
  285.9 71.9 %all-reduce.4.cloned.1.call-done = f32[16,2048]{1,0:T(8,128)} async-done(((f32[16,2048]{1,0:T(8,128)}), f32[16,2048]{1,0:T(8,128)}) %all-reduce.4.cloned.1.call-update) | async-done | bytes 131088 | tf_op jit(solution)/shard_map/psum | solution.py:92
  357.8 1.6 copy.15
  (8 shorter events, 0.1 us)
Async XLA Ops:
  7.2 85.9 %copy-start = (bf16[16,2048]{1,0:T(8,128)(2,1)S(1)}, bf16[16,2048]{1,0:T(8,128)(2,1)}, u32[]{:S(2)}) copy-start(bf16[16,2048]{1,0:T(8,128)(2,1)} %param.9) | copy-start | bytes 196612
  7.2 85.9 %all-gather.2.cloned.1.call-start = ((), (), s32[]{:S(2)}) async-start(), calls=%async_computation.2 | async-start | bytes 5242880 | tf_op jit(solution)/shard_map/all_gather | solution.py:43
  7.9 192.0 %reduce-scatter.5.cloned.1.call-start = ((), (), s32[]{:S(2)}) async-start(), calls=%async_computation.4 | async-start | bytes 81920 | tf_op jit(solution)/shard_map/reduce_scatter | solution.py:48
  97.1 104.8 %reduce-scatter.3.cloned.1.call-start = ((), (), s32[]{:S(2)}) async-start(), calls=%async_computation.3 | async-start | bytes 10485760 | tf_op jit(solution)/shard_map/reduce_scatter | solution.py:47
  111.6 115.7 %all-reduce.8.cloned.1.call-start = ((), (), s32[]{:S(2)}) async-start(), calls=%async_computation.7 | async-start | bytes 262144 | tf_op jit(solution)/shard_map/psum | solution.py:50
  111.8 4.6 %copy-start.2 = (bf16[16,2048]{1,0:T(8,128)(2,1)S(1)}, bf16[16,2048]{1,0:T(8,128)(2,1)}, u32[]{:S(2)}) copy-start(bf16[16,2048]{1,0:T(8,128)(2,1)} %param.10) | copy-start | bytes 196612
  117.3 166.9 %all-reduce.6.cloned.1.call-start = ((), (), s32[]{:S(2)}) async-start(), calls=%async_computation.6 | async-start | bytes 262144 | tf_op jit(solution)/shard_map/psum | solution.py:69
  117.3 5.9 %copy-start.5 = (s32[1,8]{1,0:T(1,128)S(1)}, s32[1,8]{1,0:T(1,128)}, u32[]{:S(2)}) copy-start(s32[1,8]{1,0:T(1,128)} %param.13) | copy-start | bytes 100
  117.4 12.7 %copy-start.4 = (f32[2048]{0:T(1024)S(1)}, f32[2048]{0:T(1024)}, u32[]{:S(2)}) copy-start(f32[2048]{0:T(1024)} %param.11) | copy-start | bytes 24580
  117.4 12.8 %copy-start.3 = (bf16[256,2048]{1,0:T(8,128)(2,1)S(1)}, bf16[256,2048]{1,0:T(8,128)(2,1)}, u32[]{:S(2)}) copy-start(bf16[256,2048]{1,0:T(8,128)(2,1)} %param.12) | copy-start | bytes 3145732
  201.8 156.0 %all-reduce.4.cloned.1.call-start = ((), (), s32[]{:S(2)}) async-start(), calls=%async_computation.5 | async-start | bytes 262144 | tf_op jit(solution)/shard_map/psum | solution.py:92
  217.8 6.1 %copy-start.1 = (bf16[256,2048]{1,0:T(8,128)(2,1)S(1)}, bf16[256,2048]{1,0:T(8,128)(2,1)}, u32[]{:S(2)}) copy-start(bf16[256,2048]{1,0:T(8,128)(2,1)} %param.7) | copy-start | bytes 3145732
Sparse Core Ops, SparseCore 0:
  9.6 83.4 all-gather.1
  97.2 18.0 reduce-scatter.4
  117.9 75.6 reduce-scatter.2
  195.8 31.4 all-reduce.7
  230.7 53.4 all-reduce.5
  288.0 69.7 all-reduce.3
where the time goes:
time: 367 us; the launch traced here: 366 us
  waiting for transfers between devices  217 us (59%)
  blocking collectives  87.8 us (24%)
  matrix products  42.5 us (12%)
  between operations  14.3 us (4%)
    all_gather x1, waiting for transfers between devices, per_device(): portion = lax.all_gather(tokens, 'col', axis=0, tiled=True)  85.1 us
    psum x1, waiting for transfers between devices, per_device(): lax.psum(row_term + first_group * norm_term, ('dp', 'col'))  71.9 us
    psum x1, blocking collectives, per_device(): backward_rows = lax.psum(padded, ('row', 'col')).astype(jnp.bfloat16)  69.2 us
    psum x1, waiting for transfers between devices, per_device(): scale_grad, bgrad_data = lax.psum((scale_terms, bgrad_terms), ('dp', 'row'))  57 us
    dot_general x8, matrix products, contract_product(): lax.dot_general(left, right, (((left_dim,), (right_dim,)), ((), ())), pre...  19.1 us
    dot_general x1, matrix products, per_device(): jnp.dot(portion, frozen_weight, preferred_element_type=jnp.float32)  14.4 us
    psum x1, blocking collectives, per_device(): scale_grad, bgrad_data = lax.psum((scale_terms, bgrad_terms), ('dp', 'row'))  12.1 us
  transfers between devices with their start and end apart: 6, of which 4 were waited for; matrix products, arithmetic and copies ran while one was open for 11% of the time, Pallas kernels for 0%

commit v1 on v0

--- a/solution.py
+++ b/solution.py
@@ -77,7 +77,7 @@
         row_index * block_rows,
         0,
     )
-    backward_rows = lax.psum(padded, ("row", "col")).astype(jnp.bfloat16)
+    backward_rows = lax.psum(lax.psum(padded, "col"), "row").astype(jnp.bfloat16)
     back_mine = lax.dynamic_slice_in_dim(backward_rows, col_index * local_rows, local_rows, 0)
     row_term = contract_product(back_mine, tokens, 0, 0)
     scaled_output_factor = (

time: 367 us -> 403 us (1.098)
  waiting for transfers between devices: 217 us -> 301 us
  blocking collectives: 87.8 us -> 38.3 us
    reduce_scatter x1, waiting for transfers between devices: 0.02 us -> 72 us  [per_device(): lax.psum_scatter(base_piece, 'row', scatter_dimension=0, tiled=True)]
    psum x1, blocking collectives: 69.2 us -> 17 us  [per_device(): lax.psum(lax.psum(padded, 'col'), 'row').astype(jnp.bfloat16)]
    all_gather x1, waiting for transfers between devices: 85.1 us -> 68.2 us  [per_device(): portion = lax.all_gather(tokens, 'col', axis=0, tiled=True)]
    psum x0 -> x1, waiting for transfers between devices: none -> 15.6 us  [per_device(): lax.psum(padded, 'col')]
    psum x1, waiting for transfers between devices: 2.4 us -> 10.2 us  [per_device(): lax.psum((norm_terms, merged_factor_terms), 'row')]
    reduce_scatter x1, waiting for transfers between devices: 0.02 us -> 5.41 us  [per_device(): lax.psum_scatter(down_portion, 'row', scatter_dimension=0, tiled=True)]
  transfers between devices with their start and end apart: 6 -> 7, of which waited for: 4 -> 7; matrix products, arithmetic and copies ran while one was open for 11% -> 11% of each run, Pallas kernels for 0% -> 0%
where the time goes in v1:
time: 403 us; the launch traced here: 402 us
  waiting for transfers between devices  301 us (75%)
  matrix products  42.6 us (11%)
  blocking collectives  38.3 us (10%)
  between operations  14.3 us (4%)
    psum x1, waiting for transfers between devices, per_device(): lax.psum(row_term + first_group * norm_term, ('dp', 'col'))  72.1 us
    reduce_scatter x1, waiting for transfers between devices, per_device(): lax.psum_scatter(base_piece, 'row', scatter_dimension=0, tiled=True)  72 us
    all_gather x1, waiting for transfers between devices, per_device(): portion = lax.all_gather(tokens, 'col', axis=0, tiled=True)  68.2 us
    psum x1, waiting for transfers between devices, per_device(): scale_grad, bgrad_data = lax.psum((scale_terms, bgrad_terms), ('dp', 'row'))  57 us
    dot_general x8, matrix products, contract_product(): lax.dot_general(left, right, (((left_dim,), (right_dim,)), ((), ())), pre...  19.2 us
    psum x1, blocking collectives, per_device(): lax.psum(lax.psum(padded, 'col'), 'row').astype(jnp.bfloat16)  17 us
    psum x1, waiting for transfers between devices, per_device(): lax.psum(padded, 'col')  15.6 us
    dot_general x1, matrix products, per_device(): jnp.dot(portion, frozen_weight, preferred_element_type=jnp.float32)  14.5 us
  transfers between devices with their start and end apart: 7, of which 7 were waited for; matrix products, arithmetic and copies ran while one was open for 11% of the time, Pallas kernels for 0%

profile of v1, /device:TPU:0, one launch (start us, length us, event | category | flops | bytes accessed | tf_op | source)
XLA Modules:
  0.0 402.4 jit_solution(1951940285349590185)
XLA Ops:
  7.2 0.0 copy-start
  7.2 0.0 all-gather.2.cloned.1.call-start
  7.2 0.7 all-gather.2.cloned.1.call-update
  7.9 0.0 all-reduce.5.cloned.1.call-start
  8.0 0.8 reduce-window.4
  8.8 0.0 copy-done
  8.8 0.0 copy-start.3
  8.8 0.0 copy-start.4
  8.8 5.9 %multiply_reduce_fusion = f32[2048]{0:T(1024)S(1)} fusion(bf16[2048,2048]{1,0:T(8,128)(2,1)} %param.8, bf16[16,2048]{1,0:T(8,128)(2,1)S(1)} %copy-done, bf16[16,2048]{1,0:T(8,128)(2,1)} %param.10), kind=kOutput, calls=%fused_computation | convolution fusion | flops 150992896 | bytes 8527872 | tf_op jit(solution)/shard_map/dot_general | solution.py:11
  14.7 8.5 %psum.49 = f32[2048]{0:T(1024)S(1)} all-reduce(f32[2048]{0:T(1024)S(1)} %multiply_reduce_fusion), channel_id=1, replica_groups=mesh['dp'=2,'row'=4,'col'=4] {'row'}, use_global_device_ids=true, to_apply=%region_3.0 | all-reduce | flops 2048 | bytes 16384 | tf_op jit(solution)/shard_map/psum | solution.py:50
  23.3 0.1 select_reduce_fusion
  23.5 0.5 convolution_dynamic-update-slice_fusion
  24.0 0.0 copy-start.2
  24.0 0.8 copy-done.2
  24.8 0.0 all-reduce.5.cloned.1.call-update
  24.8 0.0 reduce-scatter.5.cloned.1.call-start
  24.9 68.2 %all-gather.2.cloned.1.call-done = bf16[1024,2048]{1,0:T(8,128)(2,1)} async-done(((bf16[256,2048]{1,0:T(8,128)(2,1)}), bf16[1024,2048]{1,0:T(8,128)(2,1)}) %all-gather.2.cloned.1.call-update) | async-done | bytes 4194320 | tf_op jit(solution)/shard_map/all_gather | solution.py:43
  93.1 4.0 fusion.14
  97.1 0.0 reduce-scatter.5.cloned.1.call-update
  97.1 0.0 reduce-scatter.3.cloned.1.call-start
  97.1 14.5 %fusion.13 = f32[1024,2048]{1,0:T(8,128)} fusion(bf16[1024,2048]{1,0:T(8,128)(2,1)} %all-gather.2.cloned.1.call-done, bf16[2048,2048]{1,0:T(8,128)(2,1)} %param.8), kind=kOutput, calls=%fused_computation.32 | convolution fusion | flops 8589934592 | bytes 20971520 | tf_op jit(solution)/shard_map/dot_general | solution.py:44
  111.7 0.0 reduce-scatter.3.cloned.1.call-update
  111.7 0.0 all-reduce.11.cloned.1.call-start
  111.7 0.1 fusion.16
  111.9 4.6 %fusion.15 = f32[16,2048]{1,0:T(8,128)S(1)} fusion(bf16[16,2048]{1,0:T(8,128)(2,1)S(1)} %copy-done, bf16[2048,2048]{1,0:T(8,128)(2,1)} %param.8), kind=kOutput, calls=%fused_computation.34 | convolution fusion | flops 134217728 | bytes 8585216 | tf_op jit(solution)/shard_map/dot_general | solution.py:38
  116.5 0.8 convolution_add_fusion.1
  117.4 0.0 all-reduce.11.cloned.1.call-update
  117.4 0.0 all-reduce.9.cloned.1.call-start
  117.4 15.6 %all-reduce.5.cloned.1.call-done = f32[1024,16]{1,0:T(8,128)} async-done(((f32[1024,16]{1,0:T(8,128)}), f32[1024,16]{1,0:T(8,128)}) %all-reduce.5.cloned.1.call-update) | async-done | bytes 65552 | tf_op jit(solution)/shard_map/psum | solution.py:80
  133.1 17.0 %psum.52 = bf16[1024,16]{1,0:T(8,128)(2,1)S(1)} all-reduce(f32[1024,16]{1,0:T(8,128)} %all-reduce.5.cloned.1.call-done), channel_id=1, replica_groups=mesh['dp'=2,'row'=4,'col'=4] {'row'}, use_global_device_ids=true, to_apply=%region_9.10 | all-reduce | flops 16384 | bytes 98304 | tf_op jit(solution)/shard_map/psum | solution.py:80
  150.1 5.4 %reduce-scatter.5.cloned.1.call-done = f32[256,16]{0,1:T(8,128)} async-done(((f32[1024,16]{0,1:T(8,128)}), f32[256,16]{0,1:T(8,128)}) %reduce-scatter.5.cloned.1.call-update) | async-done | bytes 16400 | tf_op jit(solution)/shard_map/reduce_scatter | solution.py:48
  155.5 1.8 fusion.1
  157.3 0.0 all-reduce.9.cloned.1.call-update
  157.3 0.0 all-reduce.7.cloned.1.call-start
  157.4 72.0 %reduce-scatter.3.cloned.1.call-done = f32[256,2048]{1,0:T(8,128)} async-done(((f32[1024,2048]{1,0:T(8,128)}), f32[256,2048]{1,0:T(8,128)}) %reduce-scatter.3.cloned.1.call-update) | async-done | bytes 2097168 | tf_op jit(solution)/shard_map/reduce_scatter | solution.py:47
  229.4 3.2 multiply_reduce_fusion.1
  232.6 12.8 %psum.50 = f32[2048]{0:T(1024)S(1)} all-reduce(f32[2048]{0:T(1024)S(1)} %get-tuple-element.4), channel_id=1, replica_groups=mesh['dp'=2,'row'=4,'col'=4] {'dp','row'}, use_global_device_ids=true, to_apply=%region_7.8 | all-reduce | flops 2048 | bytes 16384 | tf_op jit(solution)/shard_map/psum | solution.py:69
  245.4 0.6 fusion.6
  246.0 5.7 %fusion.3 = f32[16,2048]{1,0:T(8,128)S(1)} fusion(bf16[2048,2048]{1,0:T(8,128)(2,1)} %param.8, bf16[16,2048]{1,0:T(8,128)(2,1)S(1)} %copy-done.3, f32[2048]{0:T(1024)S(1)} %get-tuple-element.6), kind=kOutput, calls=%fused_computation.16 | convolution fusion | flops 134316032 | bytes 8593408 | tf_op jit(solution)/shard_map/dot_general | solution.py:11
  251.7 0.1 fusion.2
  251.9 0.2 fusion
  252.1 0.9 convolution_add_fusion.3
  253.0 0.0 all-reduce.7.cloned.1.call-update
  253.1 10.2 %all-reduce.11.cloned.1.call-done = f32[16,2048]{1,0:T(8,128)} async-done(((f32[16,2048]{1,0:T(8,128)}), f32[16,2048]{1,0:T(8,128)}) %all-reduce.11.cloned.1.call-update) | async-done | bytes 131088 | tf_op jit(solution)/shard_map/psum | solution.py:50
  263.3 57.0 %all-reduce.9.cloned.1.call-done = f32[16,2048]{1,0:T(8,128)} async-done(((f32[16,2048]{1,0:T(8,128)}), f32[16,2048]{1,0:T(8,128)}) %all-reduce.9.cloned.1.call-update) | async-done | bytes 131088 | tf_op jit(solution)/shard_map/psum | solution.py:69
  320.3 1.6 multiply_add_fusion
  321.9 72.1 %all-reduce.7.cloned.1.call-done = f32[16,2048]{1,0:T(8,128)} async-done(((f32[16,2048]{1,0:T(8,128)}), f32[16,2048]{1,0:T(8,128)}) %all-reduce.7.cloned.1.call-update) | async-done | bytes 131088 | tf_op jit(solution)/shard_map/psum | solution.py:92
  394.0 1.6 copy.16
  (13 shorter events, 0.1 us)
Async XLA Ops:
  7.2 1.6 copy-start
  7.2 85.9 %all-gather.2.cloned.1.call-start = ((), (), s32[]{:S(2)}) async-start(), calls=%async_computation.2 | async-start | bytes 5242880 | tf_op jit(solution)/shard_map/all_gather | solution.py:43
  7.9 125.2 %all-reduce.5.cloned.1.call-start = ((), (), s32[]{:S(2)}) async-start(), calls=%async_computation.5 | async-start | bytes 1048576 | tf_op jit(solution)/shard_map/psum | solution.py:80
  8.8 14.5 %copy-start.6 = (s32[1,8]{1,0:T(1,128)S(1)}, s32[1,8]{1,0:T(1,128)}, u32[]{:S(2)}) copy-start(s32[1,8]{1,0:T(1,128)} %param.13) | copy-start | bytes 100
  8.8 14.6 %copy-start.5 = (f32[2048]{0:T(1024)S(1)}, f32[2048]{0:T(1024)}, u32[]{:S(2)}) copy-start(f32[2048]{0:T(1024)} %param.11) | copy-start | bytes 24580
  8.8 14.7 %copy-start.3 = (bf16[16,2048]{1,0:T(8,128)(2,1)S(1)}, bf16[16,2048]{1,0:T(8,128)(2,1)}, u32[]{:S(2)}) copy-start(bf16[16,2048]{1,0:T(8,128)(2,1)} %param.10) | copy-start | bytes 196612
  8.8 14.7 %copy-start.4 = (bf16[256,2048]{1,0:T(8,128)(2,1)S(1)}, bf16[256,2048]{1,0:T(8,128)(2,1)}, u32[]{:S(2)}) copy-start(bf16[256,2048]{1,0:T(8,128)(2,1)} %param.12) | copy-start | bytes 3145732
  24.0 0.8 copy-start.2
  24.8 130.7 %reduce-scatter.5.cloned.1.call-start = ((), (), s32[]{:S(2)}) async-start(), calls=%async_computation.4 | async-start | bytes 81920 | tf_op jit(solution)/shard_map/reduce_scatter | solution.py:48
  97.1 132.3 %reduce-scatter.3.cloned.1.call-start = ((), (), s32[]{:S(2)}) async-start(), calls=%async_computation.3 | async-start | bytes 10485760 | tf_op jit(solution)/shard_map/reduce_scatter | solution.py:47
  111.7 151.6 %all-reduce.11.cloned.1.call-start = ((), (), s32[]{:S(2)}) async-start(), calls=%async_computation.8 | async-start | bytes 262144 | tf_op jit(solution)/shard_map/psum | solution.py:50
  117.4 202.9 %all-reduce.9.cloned.1.call-start = ((), (), s32[]{:S(2)}) async-start(), calls=%async_computation.7 | async-start | bytes 262144 | tf_op jit(solution)/shard_map/psum | solution.py:69
  157.3 236.7 %all-reduce.7.cloned.1.call-start = ((), (), s32[]{:S(2)}) async-start(), calls=%async_computation.6 | async-start | bytes 262144 | tf_op jit(solution)/shard_map/psum | solution.py:92
  246.0 6.1 %copy-start.1 = (bf16[256,2048]{1,0:T(8,128)(2,1)S(1)}, bf16[256,2048]{1,0:T(8,128)(2,1)}, u32[]{:S(2)}) copy-start(bf16[256,2048]{1,0:T(8,128)(2,1)} %param.7) | copy-start | bytes 3145732
Sparse Core Ops, SparseCore 0:
  9.6 83.4 all-gather.1
  96.0 37.0 all-reduce.4
  136.1 19.3 reduce-scatter.4
  157.9 71.3 reduce-scatter.2
  231.5 31.7 all-reduce.10
  266.8 53.4 all-reduce.8
  324.2 69.7 all-reduce.6
